TPU v7x, 32 devices: a whole 2x2x4 slice. The times are simulated.
32 devices in a mesh: sub: 8 (over z, y), split: 4 (over x, core).
Axes of the slice: x: 2, y: 2, z: 4, core: 2. Of those that a mesh axis runs over, the one named last changes fastest.
Arguments:
- inv_conductance: float32 [8, 2048, 2048], P('sub', None, 'split')
- source_amp: float32 [8, 2048], P('sub', 'split'), may hold values from -6 to 6
- source_phase: float32 [8, 2048], P('sub', 'split'), may hold values from -3.140625 to 3.140625
- companion: float32 [8, 2048], P('sub', 'split'), may hold values from 0.1 to 0.8
- surge_impedance: float32 [8, 512], P('sub', 'split'), may hold values from 2 to 8
- initial_voltage: float32 [8, 64, 2048], P('sub', None, 'split'), may hold values from -6 to 6
- initial_history: float32 [8, 64, 512], P('sub', None, 'split'), may hold values from -6 to 6
- partner_sub: int32 [8, 512], P('sub', 'split'), may hold values from 0 to 7, as said below
- line_delay: int32 [8, 512], P('sub', 'split'), may hold values from 2 to 5, as said below
- open_step: int32 [8, 64, 512], P('sub', None, 'split'), may hold values from 0 to 15
Outputs:
- voltage: float32 [8, 64, 2048], P('sub', None, 'split')
- port_current: float32 [8, 64, 512], P('sub', None, 'split')
Inputs may be any that keep to these rules, and one draw needn't show every extreme that they name: partner_sub[partner_sub[s, p], p] == s and partner_sub[s, p] != s: a line joins port p of two subnetworks, both in the same block of 128 ports. At most 32 ports of one block of a subnetwork have lines to the same other subnetwork, and in every block some subnetwork gets exactly 32. `line_delay`: both ends of a line have the same delay.
All inputs are finite; a program needn't handle non-finite values.
Results may differ from a plain program's by a relative error of at most 0.00015.
Values sent between devices are 32-bit elements; how exact they have to be, the bound alone decides.
A program may use at most 64 MiB of HBM per device.

v0:
```python
import jax
import jax.numpy as jnp
from jax import lax
from jax.sharding import PartitionSpec as P

STEPS = 8
DMIN = 2


angular = 0.7


def local(
    inv_conductance,
    source_amp,
    source_phase,
    companion,
    surge_impedance,
    initial_voltage,
    initial_history,
    partner_sub,
    line_delay,
    open_step,
):
    matrix = inv_conductance[0]
    n_subs = lax.axis_size("sub")
    cont = initial_voltage.shape[1]
    nodes_dev = initial_voltage.shape[2]
    ports_dev = initial_history.shape[2]
    stride = nodes_dev // ports_dev
    capacity = max(2, 2 * ports_dev // n_subs)
    partner = partner_sub[0]
    position = jnp.arange(ports_dev, dtype=jnp.int32)
    same_far = partner[:, None] == partner[None, :]
    earlier = position[:, None] > position[None, :]
    slot_rank = jnp.sum((same_far & earlier).astype(jnp.int32), axis=1)
    target = partner * capacity + slot_rank
    routing = (target[:, None] == jnp.arange(n_subs * capacity, dtype=jnp.int32)[None, :]).astype(
        jnp.float32
    )
    amplitude = source_amp[0][None, :]
    phase = source_phase[0][None, :]
    storage = companion[0][None, :]
    impedance = surge_impedance[0][None, :]
    delays = line_delay[0][None, :]
    opens = open_step[0]
    start_history = initial_history[0]
    voltage = initial_voltage[0]
    arrived = []
    current = jnp.zeros_like(start_history)
    for step in range(STEPS):
        closed = (step < opens).astype(jnp.float32)
        history = jnp.where(step < delays, start_history, jnp.float32(0.0))
        for anchor, far_end in enumerate(arrived):
            history = jnp.where(delays == step - anchor, -far_end, history)
        inject = closed * history
        spread = jnp.concatenate(
            [inject[:, :, None], jnp.zeros((cont, ports_dev, stride - 1), jnp.float32)], 2
        ).reshape(cont, nodes_dev)
        right_side = amplitude * jnp.cos(angular * (step + 1) + phase) + storage * voltage - spread
        partial_sum = lax.dot_general(
            right_side,
            matrix,
            (((1,), (1,)), ((), ())),
            precision=lax.Precision.HIGHEST,
            preferred_element_type=jnp.float32,
        )
        voltage = lax.psum_scatter(partial_sum, "split", scatter_dimension=1, tiled=True)
        at_ports = voltage.reshape(cont, ports_dev, stride)[:, :, 0]
        current = closed * (at_ports / impedance + history)
        outgoing = closed * (2.0 * at_ports / impedance + history)
        if step + DMIN < STEPS:
            buffer = jnp.dot(outgoing, routing, precision=lax.Precision.HIGHEST)
            incoming = lax.all_to_all(buffer, "sub", split_axis=1, concat_axis=1, tiled=True)
            arrived.append(jnp.dot(incoming, routing.T, precision=lax.Precision.HIGHEST))
    return (voltage[None], current[None])


def solution(mesh):
    placed = (
        P("sub", None, "split"),
        P("sub", "split"),
        P("sub", "split"),
        P("sub", "split"),
        P("sub", "split"),
        P("sub", None, "split"),
        P("sub", None, "split"),
        P("sub", "split"),
        P("sub", "split"),
        P("sub", None, "split"),
    )
    return jax.shard_map(
        local,
        mesh=mesh,
        in_specs=placed,
        out_specs=(P("sub", None, "split"), P("sub", None, "split")),
        check_vma=False,
    )
```

profile of v0, /device:TPU:0, one launch (start us, length us, event | category | flops | bytes accessed | tf_op | source)
XLA Modules:
  0.0 328.8 jit_solution(16479804086791979434)
XLA Ops:
  8.4 1.3 reduce.7
  9.9 1.2 cosine_multiply_fusion.6
  13.5 7.2 %fusion.14 = f32[64,2048]{1,0:T(8,128)} fusion(f32[64,512]{0,1:T(8,128)S(1)} %bitcast.300, f32[1,2048,512]{2,1,0:T(8,128)} %param.10), kind=kOutput, calls=%fused_computation.14 | convolution fusion | flops 805306368 | bytes 4849664 | tf_op jit(solution)/shard_map/dot_general | solution.py:61
  21.0 24.3 %reduce-scatter.9.cloned.1.call-done = f32[64,512]{1,0:T(8,128)} async-done(((f32[64,2048]{1,0:T(8,128)}), f32[64,512]{1,0:T(8,128)}) %reduce-scatter.9.cloned.1.call-update) | async-done | bytes 131088 | tf_op jit(solution)/shard_map/reduce_scatter | solution.py:68
  46.8 12.2 %all_to_all.69 = f32[8,1,2048]{2,1,0:T(1,128)S(1)} all-to-all(f32[8,1,2048]{2,1,0:T(1,128)S(1)} %reshape.249), channel_id=1, replica_groups=mesh['sub'=8,'split'=4] {'sub'}, dimensions={0} | all-to-all | bytes 131072 | tf_op jit(solution)/shard_map/all_to_all | solution.py:74
  61.0 7.1 %fusion.12 = f32[64,2048]{1,0:T(8,128)} fusion(f32[1,2048,512]{2,1,0:T(8,128)} %param.10, f32[64,512]{1,0:T(8,128)S(1)} %copy.73, f32[64,512]{1,0:T(8,128)} %reduce-scatter.9.cloned.1.call-done, f32[512]{0:T(512)S(1)} %bitcast.347, f32[512]{0:T(512)S(1)} %bitcast.326), kind=kOutput, calls=%fused_computation.12 | convolution fusion | flops 805404672 | bytes 4984832 | tf_op jit(solution)/shard_map/dot_general | solution.py:61
  68.2 18.4 %reduce-scatter.11.cloned.1.call-done = f32[64,512]{1,0:T(8,128)} async-done(((f32[64,2048]{1,0:T(8,128)}), f32[64,512]{1,0:T(8,128)}) %reduce-scatter.11.cloned.1.call-update) | async-done | bytes 131088 | tf_op jit(solution)/shard_map/reduce_scatter | solution.py:68
  88.3 12.2 %all_to_all.70 = f32[8,1,2048]{2,1,0:T(1,128)S(1)} all-to-all(f32[8,1,2048]{2,1,0:T(1,128)S(1)} %reshape.251), channel_id=1, replica_groups=mesh['sub'=8,'split'=4] {'sub'}, dimensions={0} | all-to-all | bytes 131072 | tf_op jit(solution)/shard_map/all_to_all | solution.py:74
  102.0 7.1 %fusion.10 = f32[64,2048]{1,0:T(8,128)} fusion(f32[1,2048,512]{2,1,0:T(8,128)} %param.10, f32[64,512]{1,0:T(8,128)S(1)} %copy.78, f32[64,512]{1,0:T(8,128)} %reduce-scatter.11.cloned.1.call-done, f32[512]{0:T(512)S(1)} %bitcast.346, f32[512]{0:T(512)S(1)} %bitcast.327), kind=kOutput, calls=%fused_computation.10 | convolution fusion | flops 805404672 | bytes 4984832 | tf_op jit(solution)/shard_map/dot_general | solution.py:61
  109.2 18.3 %reduce-scatter.13.cloned.1.call-done = f32[64,512]{1,0:T(8,128)} async-done(((f32[64,2048]{1,0:T(8,128)}), f32[64,512]{1,0:T(8,128)}) %reduce-scatter.13.cloned.1.call-update) | async-done | bytes 131088 | tf_op jit(solution)/shard_map/reduce_scatter | solution.py:68
  129.2 12.2 %all_to_all.71 = f32[8,1,2048]{2,1,0:T(1,128)S(1)} all-to-all(f32[8,1,2048]{2,1,0:T(1,128)S(1)} %reshape.253), channel_id=1, replica_groups=mesh['sub'=8,'split'=4] {'sub'}, dimensions={0} | all-to-all | bytes 131072 | tf_op jit(solution)/shard_map/all_to_all | solution.py:74
  142.9 7.1 %fusion.8 = f32[64,2048]{1,0:T(8,128)} fusion(f32[1,2048,512]{2,1,0:T(8,128)} %param.10, f32[64,512]{1,0:T(8,128)S(1)} %copy.83, f32[64,512]{1,0:T(8,128)} %reduce-scatter.13.cloned.1.call-done, f32[512]{0:T(512)S(1)} %bitcast.345, f32[512]{0:T(512)S(1)} %bitcast.328), kind=kOutput, calls=%fused_computation.8 | convolution fusion | flops 805404672 | bytes 4984832 | tf_op jit(solution)/shard_map/dot_general | solution.py:61
  150.1 18.4 %reduce-scatter.15.cloned.1.call-done = f32[64,512]{1,0:T(8,128)} async-done(((f32[64,2048]{1,0:T(8,128)}), f32[64,512]{1,0:T(8,128)}) %reduce-scatter.15.cloned.1.call-update) | async-done | bytes 131088 | tf_op jit(solution)/shard_map/reduce_scatter | solution.py:68
  170.1 12.2 %all_to_all.72 = f32[8,1,2048]{2,1,0:T(1,128)S(1)} all-to-all(f32[8,1,2048]{2,1,0:T(1,128)S(1)} %reshape.255), channel_id=1, replica_groups=mesh['sub'=8,'split'=4] {'sub'}, dimensions={0} | all-to-all | bytes 131072 | tf_op jit(solution)/shard_map/all_to_all | solution.py:74
  183.9 7.1 %fusion.6 = f32[64,2048]{1,0:T(8,128)} fusion(f32[1,2048,512]{2,1,0:T(8,128)} %param.10, f32[64,512]{1,0:T(8,128)S(1)} %copy.88, f32[64,512]{1,0:T(8,128)} %reduce-scatter.15.cloned.1.call-done, f32[512]{0:T(512)S(1)} %bitcast.344, f32[512]{0:T(512)S(1)} %bitcast.329), kind=kOutput, calls=%fused_computation.6 | convolution fusion | flops 805404672 | bytes 4984832 | tf_op jit(solution)/shard_map/dot_general | solution.py:61
  191.0 18.3 %reduce-scatter.17.cloned.1.call-done = f32[64,512]{1,0:T(8,128)} async-done(((f32[64,2048]{1,0:T(8,128)}), f32[64,512]{1,0:T(8,128)}) %reduce-scatter.17.cloned.1.call-update) | async-done | bytes 131088 | tf_op jit(solution)/shard_map/reduce_scatter | solution.py:68
  211.0 12.2 %all_to_all.73 = f32[8,1,2048]{2,1,0:T(1,128)S(1)} all-to-all(f32[8,1,2048]{2,1,0:T(1,128)S(1)} %reshape.257), channel_id=1, replica_groups=mesh['sub'=8,'split'=4] {'sub'}, dimensions={0} | all-to-all | bytes 131072 | tf_op jit(solution)/shard_map/all_to_all | solution.py:74
  224.7 7.1 %fusion.4 = f32[64,2048]{1,0:T(8,128)} fusion(f32[1,2048,512]{2,1,0:T(8,128)} %param.10, f32[64,512]{1,0:T(8,128)S(1)} %copy.93, f32[64,512]{1,0:T(8,128)} %reduce-scatter.17.cloned.1.call-done, f32[512]{0:T(512)S(1)} %bitcast.343, f32[512]{0:T(512)S(1)} %bitcast.330), kind=kOutput, calls=%fused_computation.4 | convolution fusion | flops 805404672 | bytes 4984832 | tf_op jit(solution)/shard_map/dot_general | solution.py:61
  231.9 18.3 %reduce-scatter.19.cloned.1.call-done = f32[64,512]{1,0:T(8,128)} async-done(((f32[64,2048]{1,0:T(8,128)}), f32[64,512]{1,0:T(8,128)}) %reduce-scatter.19.cloned.1.call-update) | async-done | bytes 131088 | tf_op jit(solution)/shard_map/reduce_scatter | solution.py:68
  251.9 12.2 %all_to_all.74 = f32[8,1,2048]{2,1,0:T(1,128)S(1)} all-to-all(f32[8,1,2048]{2,1,0:T(1,128)S(1)} %reshape.259), channel_id=1, replica_groups=mesh['sub'=8,'split'=4] {'sub'}, dimensions={0} | all-to-all | bytes 131072 | tf_op jit(solution)/shard_map/all_to_all | solution.py:74
  265.6 7.1 %fusion.2 = f32[64,2048]{1,0:T(8,128)} fusion(f32[1,2048,512]{2,1,0:T(8,128)} %param.10, f32[64,512]{1,0:T(8,128)S(1)} %copy.98, f32[64,512]{1,0:T(8,128)} %reduce-scatter.19.cloned.1.call-done, f32[512]{0:T(512)S(1)} %bitcast.342, f32[512]{0:T(512)S(1)} %bitcast.331), kind=kOutput, calls=%fused_computation.2 | convolution fusion | flops 805404672 | bytes 4984832 | tf_op jit(solution)/shard_map/dot_general | solution.py:61
  273.1 18.1 %reduce-scatter.21.cloned.1.call-done = f32[64,512]{1,0:T(8,128)} async-done(((f32[64,2048]{1,0:T(8,128)}), f32[64,512]{1,0:T(8,128)}) %reduce-scatter.21.cloned.1.call-update) | async-done | bytes 131088 | tf_op jit(solution)/shard_map/reduce_scatter | solution.py:68
  291.2 7.1 %fusion = f32[64,2048]{1,0:T(8,128)} fusion(f32[1,2048,512]{2,1,0:T(8,128)} %param.10, f32[64,512]{1,0:T(8,128)S(1)} %copy.100, f32[64,512]{1,0:T(8,128)} %reduce-scatter.21.cloned.1.call-done, f32[512]{0:T(512)S(1)} %bitcast.332, f32[512]{0:T(512)S(1)} %bitcast.341), kind=kOutput, calls=%fused_computation | convolution fusion | flops 805404672 | bytes 4984832 | tf_op jit(solution)/shard_map/dot_general | solution.py:61
  298.3 21.8 %reduce-scatter.23.cloned.1.call-done = f32[64,512]{1,0:T(8,128)} async-done(((f32[64,2048]{1,0:T(8,128)}), f32[64,512]{1,0:T(8,128)}) %reduce-scatter.23.cloned.1.call-update) | async-done | bytes 131088 | tf_op jit(solution)/shard_map/reduce_scatter | solution.py:68
  (119 shorter events, 25.3 us)
Async XLA Ops:
  7.2 39.2 %copy-start = (f32[1,64,128]{2,1,0:T(8,128)S(1)}, f32[1,64,128]{2,1,0:T(8,128)}, u32[]{:S(2)}) copy-start(f32[1,64,128]{2,1,0:T(8,128)} %param.16) | copy-start | bytes 98308
  7.2 13.6 %copy-start.4 = (s32[1,128]{1,0:T(1,128)S(1)}, s32[1,128]{1,0:T(1,128)}, u32[]{:S(2)}) copy-start(s32[1,128]{1,0:T(1,128)} %param.17) | copy-start | bytes 1540
  7.2 39.2 %copy-start.3 = (f32[1,128]{1,0:T(1,128)S(1)}, f32[1,128]{1,0:T(1,128)}, u32[]{:S(2)}) copy-start(f32[1,128]{1,0:T(1,128)} %param.14) | copy-start | bytes 1540
  7.2 38.0 %reduce-scatter.9.cloned.1.call-start = ((), (), s32[]{:S(2)}) async-start(), calls=%async_computation.14 | async-start | bytes 655360 | tf_op jit(solution)/shard_map/reduce_scatter | solution.py:68
  12.3 48.4 %copy-start.1 = (s32[1,64,128]{2,1,0:T(8,128)S(1)}, s32[1,64,128]{2,1,0:T(8,128)}, u32[]{:S(2)}) copy-start(s32[1,64,128]{2,1,0:T(8,128)} %param.19) | copy-start | bytes 98308
  13.3 47.7 %copy-start.2 = (f32[1,512]{1,0:T(1,128)S(1)}, f32[1,512]{1,0:T(1,128)}, u32[]{:S(2)}) copy-start(f32[1,512]{1,0:T(1,128)} %param.13) | copy-start | bytes 6148
  20.7 65.9 %reduce-scatter.11.cloned.1.call-start = ((), (), s32[]{:S(2)}) async-start(), calls=%async_computation.15 | async-start | bytes 655360 | tf_op jit(solution)/shard_map/reduce_scatter | solution.py:68
  68.2 59.3 %reduce-scatter.13.cloned.1.call-start = ((), (), s32[]{:S(2)}) async-start(), calls=%async_computation.16 | async-start | bytes 655360 | tf_op jit(solution)/shard_map/reduce_scatter | solution.py:68
  109.1 59.3 %reduce-scatter.15.cloned.1.call-start = ((), (), s32[]{:S(2)}) async-start(), calls=%async_computation.17 | async-start | bytes 655360 | tf_op jit(solution)/shard_map/reduce_scatter | solution.py:68
  150.1 59.3 %reduce-scatter.17.cloned.1.call-start = ((), (), s32[]{:S(2)}) async-start(), calls=%async_computation.18 | async-start | bytes 655360 | tf_op jit(solution)/shard_map/reduce_scatter | solution.py:68
  191.0 59.3 %reduce-scatter.19.cloned.1.call-start = ((), (), s32[]{:S(2)}) async-start(), calls=%async_computation.19 | async-start | bytes 655360 | tf_op jit(solution)/shard_map/reduce_scatter | solution.py:68
  231.9 59.3 %reduce-scatter.21.cloned.1.call-start = ((), (), s32[]{:S(2)}) async-start(), calls=%async_computation.20 | async-start | bytes 655360 | tf_op jit(solution)/shard_map/reduce_scatter | solution.py:68
  272.8 47.3 %reduce-scatter.23.cloned.1.call-start = ((), (), s32[]{:S(2)}) async-start(), calls=%async_computation.21 | async-start | bytes 655360 | tf_op jit(solution)/shard_map/reduce_scatter | solution.py:68
Sparse Core Ops, SparseCore 0:
  20.8 24.3 reduce-scatter.8
  68.3 18.2 reduce-scatter.10
  109.3 18.2 reduce-scatter.12
  150.2 18.2 reduce-scatter.14
  191.1 18.1 reduce-scatter.16
  232.0 18.2 reduce-scatter.18
  272.9 18.2 reduce-scatter.20
  298.4 21.6 reduce-scatter.22
where the time goes:
time: 330 us; the launch traced here: 329 us
  waiting for transfers between devices  156 us (47%)
  blocking collectives  73.3 us (22%)
  matrix products  61 us (18%)
  between operations  14.8 us (4%)
  local copies, waits for them, and re-layouts  13.7 us (4%)
  other arithmetic  9.71 us (3%)
    reduce_scatter x8, waiting for transfers between devices, local(): lax.psum_scatter(partial_sum, 'split', scatter_dimension=1, tiled=True)  156 us
    all_to_all x6, blocking collectives, local(): lax.all_to_all(buffer, 'sub', split_axis=1, concat_axis=1, tiled=True)  73.3 us
    dot_general x8, matrix products, local(): lax.dot_general(right_side, matrix, (((1,), (1,)), ((), ())), precision=l...  57 us
    reduce_scatter x7, local copies, waits for them, and re-layouts, local(): lax.psum_scatter(partial_sum, 'split', scatter_dimension=1, tiled=True)  7.17 us
  transfers between devices with their start and end apart: 8, of which 8 were waited for; matrix products, arithmetic and copies ran while one was open for 0% of the time, Pallas kernels for 0%

commit v1 on v0

v1 whole, which is shorter than its diff:
```python
import functools

import jax
import jax.numpy as jnp
from jax import lax
from jax.experimental import pallas as pl
from jax.experimental.pallas import tpu as pltpu
from jax.sharding import PartitionSpec as P

STEPS = 8
DMIN = 2
DMAX = 5
HALVES = 2
MESH = pl.DeviceIdType.MESH

angular = 0.7
NT = (((1,), (1,)), ((), ()))
NN = (((1,), (0,)), ((), ()))


def dot(a, b, dims=NN):
    return lax.dot_general(a, b, dims, preferred_element_type=jnp.float32)


def parts_of(x, count):
    terms = []
    for _ in range(count):
        term = x.astype(jnp.bfloat16)
        terms.append(term)
        x = x - term.astype(jnp.float32)
    return terms


def exact_dot(x, onehot, dims):
    rows = x.shape[0]
    stacked = dot(jnp.concatenate(parts_of(x, 3), 0), onehot, dims)
    return (stacked[:rows] + stacked[rows : 2 * rows]) + stacked[2 * rows :]


def kernel(
    n_subs,
    inv_ref,
    amp_ref,
    phase_ref,
    comp_ref,
    surge_ref,
    volt_ref,
    hist0_ref,
    partner_ref,
    delay_ref,
    open_ref,
    out_volt_ref,
    out_cur_ref,
    mat,
    high,
    low,
    perm,
    vol,
    src,
    kept,
    outg,
    hist,
    far,
    send_a,
    send_b,
    send_c,
    recv_a,
    recv_b,
    recv_c,
    port_recv,
    load_sem,
    sems,
    psend,
    precv,
):
    sub = lax.axis_index("sub")
    me = lax.axis_index("split")
    sibling = me + 1 - 2 * lax.rem(me, 2)
    across = lax.rem(me + 2, 4)
    diagonal = lax.rem(sibling + 2, 4)
    cont = volt_ref.shape[1]
    nodes = volt_ref.shape[2]
    ports = hist0_ref.shape[2]
    stride = nodes // ports
    rows = cont // HALVES
    owners = (diagonal, across, sibling, me)

    strips = nodes // 128

    def load(slot, i):
        start = pl.multiple_of(owners[slot] * nodes, nodes)
        return pltpu.make_async_copy(
            inv_ref.at[0, pl.ds(start, nodes), pl.ds(i * 128, 128)],
            mat.at[i, pl.ds(slot * nodes, nodes), :],
            load_sem.at[slot, i],
        )

    for slot in range(4):
        for i in range(strips):
            load(slot, i).start()

    barrier = pltpu.get_barrier_semaphore()
    for other in (sibling, across):
        pl.semaphore_signal(barrier, inc=1, device_id=(sub, other), device_id_type=MESH)

    def each_peer(body):
        if n_subs <= 16:
            for j in range(1, n_subs):
                body(j)
        else:

            def step_of(j, c):
                body(j)
                return c

            lax.fori_loop(1, n_subs, step_of, 0)

    def greet(j):
        pl.semaphore_signal(
            barrier, inc=1, device_id=(lax.rem(sub + j, n_subs), me), device_id_type=MESH
        )

    each_peer(greet)

    line = lax.broadcasted_iota(jnp.int32, (nodes, nodes), 0)
    node = lax.broadcasted_iota(jnp.int32, (nodes, nodes), 1)
    wanted = (line % ports) * stride + line // ports
    perm[...] = jnp.where(node == wanted, 1.0, 0.0).astype(jnp.bfloat16)

    small = jnp.concatenate(
        [amp_ref[...], phase_ref[...], comp_ref[...], jnp.zeros((5, nodes), jnp.float32), volt_ref[0]], 0
    )
    small = exact_dot(small, perm[...], NT)
    amp, phase = small[0:1], small[1:2]
    when = (lax.broadcasted_iota(jnp.int32, (STEPS, nodes), 0) + 1).astype(jnp.float32)
    source = amp * jnp.cos(jnp.float32(angular) * when + phase)
    for step in range(STEPS):
        src[step] = source[step : step + 1]
    src[STEPS] = small[2:3]
    for half in range(HALVES):
        vol[half] = small[8 + half * rows : 8 + (half + 1) * rows]
        for early in range(DMAX):
            far[early, half] = -hist0_ref[0, half * rows : (half + 1) * rows, :]

    def prepare(slot, c):
        base = pl.multiple_of(slot * nodes, nodes)
        for j in range(stride):
            chunk = jnp.concatenate(
                [
                    mat[i, pl.ds(base + j, ports, stride=stride), :]
                    for i in range(strips)
                ],
                1,
            )
            top, rest = parts_of(chunk, 2)
            cols = pl.ds(j * ports, ports)
            high[slot, :, cols] = dot(perm[...], top, NT).astype(jnp.bfloat16)
            low[slot, :, cols] = dot(perm[...], rest, NT).astype(jnp.bfloat16)
        return c

    for slot in range(4):
        for i in range(strips):
            load(slot, i).wait()
    lax.fori_loop(0, 4, prepare, 0)

    pl.semaphore_wait(barrier, n_subs + 1)

    def remote(kind, t, half):
        source_ref, target_ref, device = (
            (send_a, recv_a, sibling),
            (send_b, recv_b, sibling),
            (send_c, recv_c, across),
        )[kind]
        return pltpu.make_async_remote_copy(
            src_ref=source_ref.at[t, half],
            dst_ref=target_ref.at[t, half],
            send_sem=sems.at[0, kind, t, half],
            recv_sem=sems.at[1, kind, t, half],
            device_id=(sub, device),
            device_id_type=MESH,
        )

    impedance = surge_ref[...]
    partner = partner_ref[...]
    delays = delay_ref[...]

    def all_ports(t, half, sem):
        return pltpu.make_async_copy(port_recv.at[t, half], port_recv.at[t, half], sem.at[t, half])

    def opened(t, half):
        return t < open_ref[0, half * rows : (half + 1) * rows, :]

    def finish(t, half):
        remote(1, t, half).wait_recv()
        remote(2, t, half).wait_recv()
        done = kept[half] + recv_b[t, half] + recv_c[t, half]
        vol[half] = done
        return done

    def ports_out(t, half, done):
        ratio = done[:, :ports] / impedance
        value = jnp.where(opened(t, half), 2.0 * ratio + hist[half], 0.0)
        outg[t, half] = value

        def send(j):
            pltpu.make_async_remote_copy(
                src_ref=outg.at[t, half],
                dst_ref=port_recv.at[t, half, j - 1],
                send_sem=psend.at[t, half],
                recv_sem=precv.at[t, half],
                device_id=(lax.rem(sub + j, n_subs), me),
                device_id_type=MESH,
            ).start()

        each_peer(send)

    def ports_in(t, half):
        all_ports(t, half, precv).wait()

        def pick(j, total):
            origin = lax.rem(sub + n_subs - j, n_subs)
            return jnp.where(partner == origin, port_recv[t, half, j - 1], total)

        total = jnp.zeros((rows, ports), jnp.float32)
        if n_subs <= 16:
            for j in range(1, n_subs):
                total = pick(j, total)
        else:
            total = lax.fori_loop(1, n_subs, pick, total)
        far[t + DMAX, half] = total

    def step_of(t, c):
        for half in range(HALVES):

            @pl.when(t >= 1)
            def _():
                done = finish(t - 1, half)

                @pl.when(t - 1 + DMIN < STEPS)
                def _():
                    ports_out(t - 1, half, done)

            @pl.when(t >= DMIN)
            def _():
                ports_in(t - DMIN, half)

            history = jnp.zeros((rows, ports), jnp.float32)
            for d in range(DMIN, DMAX + 1):
                history = jnp.where(delays == d, -far[t - d + DMAX, half], history)
            hist[half] = history
            inject = jnp.where(opened(t, half), history, 0.0)
            right = src[t] + src[STEPS] * vol[half]
            right = jnp.concatenate([right[:, :ports] - inject, right[:, ports:]], 1)
            both = jnp.concatenate(parts_of(right, 2), 0)

            def product(slot):
                twice = dot(both, high[slot])
                return (twice[:rows] + twice[rows:]) + dot(both[:rows], low[slot])

            send_a[t, half] = product(0)
            remote(0, t, half).start()
            mine = product(1)
            send_b[t, half] = product(2)
            remote(1, t, half).start()
            kept[half] = product(3)
            remote(0, t, half).wait_recv()
            send_c[t, half] = mine + recv_a[t, half]
            remote(2, t, half).start()
        return c

    lax.fori_loop(0, STEPS, step_of, 0)

    last = STEPS - 1
    for half in range(HALVES):
        done = finish(last, half)
        span = slice(half * rows, (half + 1) * rows)
        ratio = done[:, :ports] / impedance
        out_cur_ref[0, span, :] = jnp.where(opened(last, half), ratio + hist[half], 0.0)
        out_volt_ref[0, span, :] = exact_dot(done, perm[...], NN)

    def drain(t, c):
        for half in range(HALVES):
            for kind in range(3):
                remote(kind, t, half).wait_send()

            @pl.when(t + DMIN < STEPS)
            def _():
                all_ports(t, half, psend).wait()

        return c

    lax.fori_loop(0, STEPS, drain, 0)


def local(*args):
    n_subs = lax.axis_size("sub")
    volt, hist0 = args[5], args[6]
    cont, nodes = volt.shape[1], volt.shape[2]
    ports = hist0.shape[2]
    rows = cont // HALVES
    f32, bf16 = jnp.float32, jnp.bfloat16
    block = (STEPS, HALVES, rows, nodes)
    vmem = pl.BlockSpec(memory_space=pltpu.VMEM)
    moves = STEPS - DMIN
    dma = pltpu.SemaphoreType.DMA
    return pl.pallas_call(
        functools.partial(kernel, n_subs),
        out_shape=(
            jax.ShapeDtypeStruct(volt.shape, f32),
            jax.ShapeDtypeStruct(hist0.shape, f32),
        ),
        in_specs=[pl.BlockSpec(memory_space=pl.ANY)] + [vmem] * 9,
        out_specs=(vmem, vmem),
        scratch_shapes=[
            pltpu.VMEM((nodes // 128, 4 * nodes, 128), f32),
            pltpu.VMEM((4, nodes, nodes), bf16),
            pltpu.VMEM((4, nodes, nodes), bf16),
            pltpu.VMEM((nodes, nodes), bf16),
            pltpu.VMEM((HALVES, rows, nodes), f32),
            pltpu.VMEM((STEPS + 1, 1, nodes), f32),
            pltpu.VMEM((HALVES, rows, nodes), f32),
            pltpu.VMEM((moves, HALVES, rows, ports), f32),
            pltpu.VMEM((HALVES, rows, ports), f32),
            pltpu.VMEM((STEPS + DMAX, HALVES, rows, ports), f32),
            pltpu.VMEM(block, f32),
            pltpu.VMEM(block, f32),
            pltpu.VMEM(block, f32),
            pltpu.VMEM(block, f32),
            pltpu.VMEM(block, f32),
            pltpu.VMEM(block, f32),
            pltpu.VMEM((moves, HALVES, n_subs - 1, rows, ports), f32),
            dma((4, nodes // 128)),
            dma((2, 3, STEPS, HALVES)),
            dma((moves, HALVES)),
            dma((moves, HALVES)),
        ],
        compiler_params=pltpu.CompilerParams(
            collective_id=0, has_side_effects=True, vmem_limit_bytes=62 * 1024 * 1024
        ),
    )(*args)


def solution(mesh):
    placed = (
        P("sub", None, "split"),
        P("sub", "split"),
        P("sub", "split"),
        P("sub", "split"),
        P("sub", "split"),
        P("sub", None, "split"),
        P("sub", None, "split"),
        P("sub", "split"),
        P("sub", "split"),
        P("sub", None, "split"),
    )
    return jax.shard_map(
        local,
        mesh=mesh,
        in_specs=placed,
        out_specs=(P("sub", None, "split"), P("sub", None, "split")),
        check_vma=False,
    )
```

time: 330 us -> 63.2 us (0.19)
  waiting for transfers between devices: 156 us -> 0 us
  blocking collectives: 73.3 us -> 0 us
  matrix products: 61 us -> 0 us
  Pallas kernels: 0 us -> 59.4 us
  between operations: 14.8 us -> 0.64 us
  local copies, waits for them, and re-layouts: 13.7 us -> 2.94 us
  other arithmetic: 9.71 us -> 0 us
    reduce_scatter x8 -> x0, waiting for transfers between devices: 156 us -> none  [local(): lax.psum_scatter(partial_sum, 'split', scatter_dimension=1, tiled=True)]
    all_to_all x6 -> x0, blocking collectives: 73.3 us -> none  [local(): lax.all_to_all(buffer, 'sub', split_axis=1, concat_axis=1, tiled=True)]
    dot_general x20 -> x0, matrix products: 61 us -> none  [the longest x8 57 us: local(): lax.dot_general(right_side, matrix, (((1,), (1,)), ((), ())), precision=l...]
    pallas_call x0 -> x1, Pallas kernels: none -> 59.4 us  [local(): pl.pallas_call(functools.partial(kernel, n_subs), out_shape=(jax.ShapeDty...]
    reduce_scatter x7 -> x0, local copies, waits for them, and re-layouts: 7.17 us -> none  [local(): lax.psum_scatter(partial_sum, 'split', scatter_dimension=1, tiled=True)]
    all_to_all x6 -> x0, other arithmetic: 4.79 us -> none  [local(): lax.all_to_all(buffer, 'sub', split_axis=1, concat_axis=1, tiled=True)]
  transfers between devices with their start and end apart: 8 -> 0, of which waited for: 8 -> 0; matrix products, arithmetic and copies ran while one was open for 0% -> 0% of each run, Pallas kernels for 0% -> 0%
where the time goes in v1:
time: 63.2 us; the launch traced here: 62.9 us
  Pallas kernels  59.4 us (94%)
  local copies, waits for them, and re-layouts  2.94 us (5%)
  between operations  0.64 us (1%)
    pallas_call x1, Pallas kernels, local(): pl.pallas_call(functools.partial(kernel, n_subs), out_shape=(jax.ShapeDty...  59.4 us
    unnamed x2, local copies, waits for them, and re-layouts  2.94 us

profile of v1, /device:TPU:0, one launch (start us, length us, event | category | flops | bytes accessed | tf_op | source)
XLA Modules:
  0.0 62.9 jit_solution(2730798833080711857)
XLA Ops:
  0.6 59.4 %shard_map.113 = (f32[1,64,512]{2,1,0:T(8,128)}, f32[1,64,128]{2,1,0:T(8,128)}) custom-call(f32[1,2048,512]{2,1,0:T(8,128)} %inv_ref.1, f32[1,512]{1,0:T(1,128)} %amp_ref.1, f32[1,512]{1,0:T(1,128)} %phase_ref.1, f32[1,512]{1,0:T(1,128)} %comp_ref.1, f32[1,128]{1,0:T(1,128)} %surge_ref.1, f32[1,64,512]{2,1,0:T(8,128)} %volt_ref.1, f32[1,64,128]{2,1,0:T(8,128)} %hist0_ref.1, ...), custom_call_target="tpu_custom_call" | custom-call | tf_op jit(solution)/shard_map/pallas_call | solution.py:306
  60.0 1.6 %copy.14 = f32[1,64,512]{2,1,0:T(8,128)} copy(f32[1,64,512]{2,1,0:T(8,128)} %get-tuple-element.4) | data formatting | bytes 262144
  61.6 1.4 %copy.15 = f32[1,64,128]{2,1,0:T(8,128)} copy(f32[1,64,128]{2,1,0:T(8,128)} %get-tuple-element.5) | data formatting | bytes 65536

commit v2 on v1

--- a/solution.py
+++ b/solution.py
@@ -11,6 +11,8 @@
 DMIN = 2
 DMAX = 5
 HALVES = 2
+GROUPS = 2
+LAG = 0
 MESH = pl.DeviceIdType.MESH
 
 angular = 0.7
@@ -29,6 +31,13 @@
         terms.append(term)
         x = x - term.astype(jnp.float32)
     return terms
+
+
+def packing(n_subs, ports, cont):
+    capacity = max(2, 2 * ports // n_subs)
+    lanes = ports // capacity
+    fits = n_subs * ports <= 1024 and (cont // GROUPS) % (8 * lanes) == 0
+    return fits and ports % capacity == 0, capacity, lanes
 
 
 def exact_dot(x, onehot, dims):
@@ -58,6 +67,10 @@
     vol,
     src,
     kept,
+    mine,
+    value,
+    spread,
+    gather,
     outg,
     hist,
     far,
@@ -83,6 +96,9 @@
     ports = hist0_ref.shape[2]
     stride = nodes // ports
     rows = cont // HALVES
+    per = HALVES // GROUPS
+    wide = cont // GROUPS
+    packed, capacity, lanes = packing(n_subs, ports, cont)
     owners = (diagonal, across, sibling, me)
 
     strips = nodes // 128
@@ -139,11 +155,38 @@
     src[STEPS] = small[2:3]
     for half in range(HALVES):
         vol[half] = small[8 + half * rows : 8 + (half + 1) * rows]
+
+    for group in range(GROUPS):
         for early in range(DMAX):
-            far[early, half] = -hist0_ref[0, half * rows : (half + 1) * rows, :]
+            far[early, group] = -hist0_ref[0, group * wide : (group + 1) * wide, :]
+
+    partner = partner_ref[...]
+    if packed:
+        across_row = jnp.broadcast_to(partner.astype(jnp.float32), (ports, ports))
+        down = across_row.T
+        up = lax.broadcasted_iota(jnp.int32, (ports, ports), 0)
+        right_of = lax.broadcasted_iota(jnp.int32, (ports, ports), 1)
+        same = jnp.where(across_row == down, 1.0, 0.0)
+        rank_row = jnp.sum(jnp.where(up < right_of, same, 0.0), axis=0, keepdims=True)
+        rank_col = jnp.sum(jnp.where(right_of < up, same, 0.0), axis=1, keepdims=True)
+        slot_row = across_row[:1] * capacity + rank_row
+        slot_col = down * capacity + rank_col
+        for q in range(n_subs):
+            base = q * capacity
+            want_col = (base + right_of % capacity).astype(jnp.float32)
+            hit_col = jnp.where(slot_col == want_col, 1.0, 0.0)
+            want_row = (base + up % capacity).astype(jnp.float32)
+            hit_row = jnp.where(slot_row == want_row, 1.0, 0.0)
+            for g in range(lanes):
+                spread[g * ports : (g + 1) * ports, q * ports : (q + 1) * ports] = jnp.where(
+                    right_of // capacity == g, hit_col, 0.0
+                ).astype(jnp.bfloat16)
+                gather[q * ports : (q + 1) * ports, g * ports : (g + 1) * ports] = jnp.where(
+                    up // capacity == g, hit_row, 0.0
+                ).astype(jnp.bfloat16)
 
     def prepare(slot, c):
-        base = pl.multiple_of(slot * nodes, nodes)
+        base = slot * nodes
         for j in range(stride):
             chunk = jnp.concatenate(
                 [
@@ -161,7 +204,7 @@
     for slot in range(4):
         for i in range(strips):
             load(slot, i).wait()
-    lax.fori_loop(0, 4, prepare, 0)
+        prepare(slot, 0)
 
     pl.semaphore_wait(barrier, n_subs + 1)
 
@@ -181,11 +224,12 @@
         )
 
     impedance = surge_ref[...]
-    partner = partner_ref[...]
     delays = delay_ref[...]
 
-    def all_ports(t, half, sem):
-        return pltpu.make_async_copy(port_recv.at[t, half], port_recv.at[t, half], sem.at[t, half])
+    def all_ports(t, group, sem):
+        return pltpu.make_async_copy(
+            port_recv.at[t, group], port_recv.at[t, group], sem.at[t, group]
+        )
 
     def opened(t, half):
         return t < open_ref[0, half * rows : (half + 1) * rows, :]
@@ -197,75 +241,116 @@
         vol[half] = done
         return done
 
-    def ports_out(t, half, done):
+    def outgoing(t, half, done):
         ratio = done[:, :ports] / impedance
-        value = jnp.where(opened(t, half), 2.0 * ratio + hist[half], 0.0)
-        outg[t, half] = value
+        within = half % per * rows
+        value[half // per, within : within + rows] = jnp.where(
+            opened(t, half), 2.0 * ratio + hist[half], 0.0
+        )
+
+    def ports_out(t, group):
+        if packed:
+            tall = value[group]
+            high_rows = wide // lanes
+            flat = jnp.concatenate(
+                [tall[g * high_rows : (g + 1) * high_rows] for g in range(lanes)], 1
+            )
+            sent = exact_dot(flat, spread[...], NN)
+            for q in range(n_subs):
+                outg[t, group, q] = sent[:, q * ports : (q + 1) * ports]
+        else:
+            outg[t, group, 0] = value[group]
 
         def send(j):
+            peer = lax.rem(sub + j, n_subs)
             pltpu.make_async_remote_copy(
-                src_ref=outg.at[t, half],
-                dst_ref=port_recv.at[t, half, j - 1],
-                send_sem=psend.at[t, half],
-                recv_sem=precv.at[t, half],
-                device_id=(lax.rem(sub + j, n_subs), me),
+                src_ref=outg.at[t, group, peer if packed else 0],
+                dst_ref=port_recv.at[t, group, j - 1],
+                send_sem=psend.at[t, group],
+                recv_sem=precv.at[t, group],
+                device_id=(peer, me),
                 device_id_type=MESH,
             ).start()
 
         each_peer(send)
 
-    def ports_in(t, half):
-        all_ports(t, half, precv).wait()
-
-        def pick(j, total):
-            origin = lax.rem(sub + n_subs - j, n_subs)
-            return jnp.where(partner == origin, port_recv[t, half, j - 1], total)
-
-        total = jnp.zeros((rows, ports), jnp.float32)
-        if n_subs <= 16:
-            for j in range(1, n_subs):
-                total = pick(j, total)
+    def ports_in(t, group):
+        all_ports(t, group, precv).wait()
+        if packed:
+            pieces = []
+            for q in range(n_subs):
+                j = lax.rem(sub + n_subs - q, n_subs)
+                block = port_recv[t, group, jnp.maximum(j - 1, 0)]
+                pieces.append(block)
+            flat = exact_dot(jnp.concatenate(pieces, 1), gather[...], NN)
+            total = jnp.concatenate(
+                [flat[:, g * ports : (g + 1) * ports] for g in range(lanes)], 0
+            )
         else:
-            total = lax.fori_loop(1, n_subs, pick, total)
-        far[t + DMAX, half] = total
-
-    def step_of(t, c):
-        for half in range(HALVES):
-
-            @pl.when(t >= 1)
-            def _():
-                done = finish(t - 1, half)
-
-                @pl.when(t - 1 + DMIN < STEPS)
-                def _():
-                    ports_out(t - 1, half, done)
+
+            def pick(j, total):
+                origin = lax.rem(sub + n_subs - j, n_subs)
+                return jnp.where(partner == origin, port_recv[t, group, j - 1], total)
+
+            total = jnp.zeros((wide, ports), jnp.float32)
+            if n_subs <= 16:
+                for j in range(1, n_subs):
+                    total = pick(j, total)
+            else:
+                total = lax.fori_loop(1, n_subs, pick, total)
+        far[t + DMAX, group] = total
+
+    def begin(t, half):
+        group, place = half // per, half % per
+        within = slice(place * rows, (place + 1) * rows)
+
+        @pl.when(t >= 1)
+        def _():
+            outgoing(t - 1, half, finish(t - 1, half))
+
+        if place == 0:
 
             @pl.when(t >= DMIN)
             def _():
-                ports_in(t - DMIN, half)
-
-            history = jnp.zeros((rows, ports), jnp.float32)
-            for d in range(DMIN, DMAX + 1):
-                history = jnp.where(delays == d, -far[t - d + DMAX, half], history)
-            hist[half] = history
-            inject = jnp.where(opened(t, half), history, 0.0)
-            right = src[t] + src[STEPS] * vol[half]
-            right = jnp.concatenate([right[:, :ports] - inject, right[:, ports:]], 1)
-            both = jnp.concatenate(parts_of(right, 2), 0)
-
-            def product(slot):
-                twice = dot(both, high[slot])
-                return (twice[:rows] + twice[rows:]) + dot(both[:rows], low[slot])
-
-            send_a[t, half] = product(0)
-            remote(0, t, half).start()
-            mine = product(1)
-            send_b[t, half] = product(2)
-            remote(1, t, half).start()
-            kept[half] = product(3)
-            remote(0, t, half).wait_recv()
-            send_c[t, half] = mine + recv_a[t, half]
-            remote(2, t, half).start()
+                ports_in(t - DMIN, group)
+
+        history = jnp.zeros((rows, ports), jnp.float32)
+        for d in range(DMIN, DMAX + 1):
+            history = jnp.where(delays == d, -far[t - d + DMAX, group, within], history)
+        hist[half] = history
+        inject = jnp.where(opened(t, half), history, 0.0)
+        right = src[t] + src[STEPS] * vol[half]
+        right = jnp.concatenate([right[:, :ports] - inject, right[:, ports:]], 1)
+        both = jnp.concatenate(parts_of(right, 2), 0)
+
+        def product(slot):
+            twice = dot(both, high[slot])
+            return (twice[:rows] + twice[rows:]) + dot(both[:rows], low[slot])
+
+        send_a[t, half] = product(0)
+        remote(0, t, half).start()
+        if place == per - 1:
+
+            @pl.when((t >= 1) & (t - 1 + DMIN < STEPS))
+            def _():
+                ports_out(t - 1, group)
+
+        send_b[t, half] = product(2)
+        remote(1, t, half).start()
+        mine[half] = product(1)
+        kept[half] = product(3)
+
+    def relay(t, half):
+        remote(0, t, half).wait_recv()
+        send_c[t, half] = mine[half] + recv_a[t, half]
+        remote(2, t, half).start()
+
+    def step_of(t, c):
+        for turn in range(HALVES + LAG):
+            if turn < HALVES:
+                begin(t, turn)
+            if turn >= LAG:
+                relay(t, turn - LAG)
         return c
 
     lax.fori_loop(0, STEPS, step_of, 0)
@@ -283,9 +368,10 @@
             for kind in range(3):
                 remote(kind, t, half).wait_send()
 
-            @pl.when(t + DMIN < STEPS)
-            def _():
-                all_ports(t, half, psend).wait()
+        @pl.when(t + DMIN < STEPS)
+        def _():
+            for group in range(GROUPS):
+                all_ports(t, group, psend).wait()
 
         return c
 
@@ -302,6 +388,10 @@
     block = (STEPS, HALVES, rows, nodes)
     vmem = pl.BlockSpec(memory_space=pltpu.VMEM)
     moves = STEPS - DMIN
+    wide = cont // GROUPS
+    packed, _, lanes = packing(n_subs, ports, cont)
+    port_rows = wide // lanes if packed else wide
+    blocks = n_subs if packed else 1
     dma = pltpu.SemaphoreType.DMA
     return pl.pallas_call(
         functools.partial(kernel, n_subs),
@@ -319,20 +409,24 @@
             pltpu.VMEM((HALVES, rows, nodes), f32),
             pltpu.VMEM((STEPS + 1, 1, nodes), f32),
             pltpu.VMEM((HALVES, rows, nodes), f32),
-            pltpu.VMEM((moves, HALVES, rows, ports), f32),
+            pltpu.VMEM((HALVES, rows, nodes), f32),
+            pltpu.VMEM((GROUPS, wide, ports), f32),
+            pltpu.VMEM((lanes * ports, n_subs * ports) if packed else (16, 128), bf16),
+            pltpu.VMEM((n_subs * ports, lanes * ports) if packed else (16, 128), bf16),
+            pltpu.VMEM((moves, GROUPS, blocks, port_rows, ports), f32),
             pltpu.VMEM((HALVES, rows, ports), f32),
-            pltpu.VMEM((STEPS + DMAX, HALVES, rows, ports), f32),
-            pltpu.VMEM(block, f32),
-            pltpu.VMEM(block, f32),
-            pltpu.VMEM(block, f32),
-            pltpu.VMEM(block, f32),
-            pltpu.VMEM(block, f32),
-            pltpu.VMEM(block, f32),
-            pltpu.VMEM((moves, HALVES, n_subs - 1, rows, ports), f32),
+            pltpu.VMEM((STEPS + DMAX, GROUPS, wide, ports), f32),
+            pltpu.VMEM(block, f32),
+            pltpu.VMEM(block, f32),
+            pltpu.VMEM(block, f32),
+            pltpu.VMEM(block, f32),
+            pltpu.VMEM(block, f32),
+            pltpu.VMEM(block, f32),
+            pltpu.VMEM((moves, GROUPS, n_subs - 1, port_rows, ports), f32),
             dma((4, nodes // 128)),
             dma((2, 3, STEPS, HALVES)),
-            dma((moves, HALVES)),
-            dma((moves, HALVES)),
+            dma((moves, GROUPS)),
+            dma((moves, GROUPS)),
         ],
         compiler_params=pltpu.CompilerParams(
             collective_id=0, has_side_effects=True, vmem_limit_bytes=62 * 1024 * 1024

time: 63.2 us -> 59.4 us (0.940)
  Pallas kernels: 59.4 us -> 55.6 us
    pallas_call x1, Pallas kernels: 59.4 us -> 55.6 us  [local(): pl.pallas_call(functools.partial(kernel, n_subs), out_shape=(jax.ShapeDty...]
where the time goes in v2:
time: 59.4 us; the launch traced here: 59.2 us
  Pallas kernels  55.6 us (94%)
  local copies, waits for them, and re-layouts  2.94 us (5%)
  between operations  0.64 us (1%)
    pallas_call x1, Pallas kernels, local(): pl.pallas_call(functools.partial(kernel, n_subs), out_shape=(jax.ShapeDty...  55.6 us
    unnamed x2, local copies, waits for them, and re-layouts  2.94 us

profile of v2, /device:TPU:0, one launch (start us, length us, event | category | flops | bytes accessed | tf_op | source)
XLA Modules:
  0.0 59.2 jit_solution(2295843798684432515)
XLA Ops:
  0.6 55.6 %shard_map.113 = (f32[1,64,512]{2,1,0:T(8,128)}, f32[1,64,128]{2,1,0:T(8,128)}) custom-call(f32[1,2048,512]{2,1,0:T(8,128)} %inv_ref.1, f32[1,512]{1,0:T(1,128)} %amp_ref.1, f32[1,512]{1,0:T(1,128)} %phase_ref.1, f32[1,512]{1,0:T(1,128)} %comp_ref.1, f32[1,128]{1,0:T(1,128)} %surge_ref.1, f32[1,64,512]{2,1,0:T(8,128)} %volt_ref.1, f32[1,64,128]{2,1,0:T(8,128)} %hist0_ref.1, ...), custom_call_target="tpu_custom_call" | custom-call | tf_op jit(solution)/shard_map/pallas_call | solution.py:396
  56.2 1.6 %copy.14 = f32[1,64,512]{2,1,0:T(8,128)} copy(f32[1,64,512]{2,1,0:T(8,128)} %get-tuple-element.4) | data formatting | bytes 262144
  57.8 1.4 %copy.15 = f32[1,64,128]{2,1,0:T(8,128)} copy(f32[1,64,128]{2,1,0:T(8,128)} %get-tuple-element.5) | data formatting | bytes 65536
